TPU v7x, 32 devices: a whole 2x2x4 slice. The times are simulated.
32 devices in a mesh: expert: 4 (over x, core), shard: 8 (over z, y).
Axes of the slice: x: 2, y: 2, z: 4, core: 2. Of those that a mesh axis runs over, the one named last changes fastest.
Arguments:
- tokens: bfloat16 [48, 4096], P('shard', 'expert'), may hold values from -6 to 6
- expert_ids: int32 [48, 2], P('shard'), may hold values from 0 to 3, all different within a row; in each aligned block of 6 rows (0 to 5, 6 to 11, ...) at most 6 rows name the same one
- gates: float32 [48, 2], P('shard'), may hold values from 0.1 to 1
- gate_proj: bfloat16 [4, 4096, 8192], P('expert', None, 'shard'), may hold values from -0.09375 to 0.09375
- up_proj: bfloat16 [4, 4096, 8192], P('expert', None, 'shard'), may hold values from -0.09375 to 0.09375
- down_proj_t: bfloat16 [4, 4096, 8192], P('expert', 'shard'), may hold values from -0.0625 to 0.0625
Outputs:
- mixed: bfloat16 [48, 4096], P('shard', 'expert')
Inputs may be any that keep to these rules, and one draw needn't show every extreme that they name: `expert_ids`: each token names two different experts; among the 6 tokens of one aligned block no expert is named more than 6 times, and in every draw some expert is named exactly 6 times in some block.
All inputs are finite; a program needn't handle non-finite values.
Results may differ from a plain program's by a relative error of at most 0.0085.
Values may be sent and summed in bfloat16 or wider, within the bound.
A program may use at most 64 MiB of HBM per device.

v0:
```python
import jax
import jax.numpy as jnp
from jax import lax
from jax.sharding import PartitionSpec as P


def shards(tokens, expert_ids, gates, gate_proj, up_proj, down_proj_t):
    experts = lax.axis_size("expert")
    own_expert = lax.axis_index("expert")
    tok_count = tokens.shape[0]
    capacity = min(tok_count, 4 * tok_count // experts)
    expert_range = jnp.arange(experts, dtype=jnp.int32)
    matches = expert_ids[:, :, None] == expert_range[None, None, :]
    routed = jnp.sum(matches.astype(jnp.int32), axis=1)
    weight = jnp.sum(gates[:, :, None] * matches.astype(jnp.float32), axis=1)
    slot_rank = jnp.cumsum(routed, axis=0) - routed
    slot_range = jnp.arange(capacity, dtype=jnp.int32)
    selector = (slot_rank.T[:, None, :] == slot_range[None, :, None]) & (routed.T[:, None, :] > 0)
    selector_bf = selector.astype(jnp.bfloat16)
    whole = lax.all_gather(tokens, "expert", axis=1, tiled=True)
    own_select = lax.dynamic_index_in_dim(selector_bf, own_expert, 0, keepdims=False)
    own_rows = jnp.dot(own_select, whole, preferred_element_type=jnp.float32).astype(jnp.bfloat16)
    gate_local = gate_proj[0]
    up_local = up_proj[0]
    down_local = down_proj_t[0]
    piece = lax.all_gather(own_rows, "shard", axis=0, tiled=True)
    gate_out = jnp.dot(piece, gate_local, preferred_element_type=jnp.float32)
    up_out = jnp.dot(piece, up_local, preferred_element_type=jnp.float32)
    hidden = (jax.nn.silu(gate_out) * up_out).astype(jnp.bfloat16)
    out_columns = lax.dot_general(
        lax.all_gather(hidden, "shard", axis=1, tiled=True),
        down_local,
        (((1,), (1,)), ((), ())),
        preferred_element_type=jnp.float32,
    )
    expert_out = lax.all_to_all(
        out_columns.astype(jnp.bfloat16), "shard", split_axis=0, concat_axis=1, tiled=True
    )
    gathered_out = lax.all_to_all(expert_out, "expert", split_axis=1, concat_axis=0, tiled=True)
    combiner = (
        (selector.astype(jnp.float32) * weight.T[:, None, :])
        .reshape(experts * capacity, tok_count)
        .T
    )
    mixed_sum = jnp.dot(combiner, gathered_out.astype(jnp.float32), precision=lax.Precision.HIGHEST)
    return mixed_sum.astype(jnp.bfloat16)


def solution(mesh):
    in_specs = (
        P("shard", "expert"),
        P("shard", None),
        P("shard", None),
        P("expert", None, "shard"),
        P("expert", None, "shard"),
        P("expert", "shard", None),
    )
    out_specs = P("shard", "expert")
    return jax.shard_map(shards, mesh=mesh, in_specs=in_specs, out_specs=out_specs, check_vma=False)
```

profile of v0, /device:TPU:0, one launch (start us, length us, event | category | flops | bytes accessed | tf_op | source)
XLA Modules:
  0.0 105.6 jit_solution(6960518200582428909)
XLA Ops:
  0.0 0.7 convert_reduce_fusion
  0.7 0.2 reduce_window_sum.11
  0.9 6.4 %all_gather.9 = bf16[6,4096]{1,0:T(8,128)(2,1)S(1)} all-gather(bf16[6,1024]{1,0:T(8,128)(2,1)} %param.6), channel_id=1, replica_groups=mesh['expert'=4,'shard'=8] {'expert'}, dimensions={1}, use_global_device_ids=true | all-gather | bytes 61440 | tf_op jit(solution)/shard_map/all_gather | solution.py:20
  7.3 0.1 fusion.6
  7.5 32.4 %all-gather = bf16[8,6,4096]{2,1,0:T(8,128)(2,1)S(1)} all-gather(bf16[1,6,4096]{2,1,0:T(8,128)(2,1)S(1)} %fusion.6), channel_id=1, replica_groups=mesh['expert'=4,'shard'=8] {'shard'}, dimensions={0}, use_global_device_ids=true | all-gather | bytes 442368 | tf_op jit(solution)/shard_map/all_gather | solution.py:26
  39.9 0.1 reshape.15
  40.0 0.0 slice-start
  40.0 5.1 %fusion.4 = f32[48,1024]{1,0:T(8,128)S(1)} fusion(bf16[48,4096]{1,0:T(8,128)(2,1)S(1)} %reshape.15, bf16[1,4096,1024]{2,1,0:T(8,128)(2,1)} %param.9), kind=kOutput, calls=%fused_computation.4 | convolution fusion | flops 402653184 | bytes 8978432 | tf_op jit(solution)/shard_map/dot_general | solution.py:27
  45.1 0.0 slice-start.1
  45.1 5.1 %fusion.10 = bf16[48,1024]{1,0:T(8,128)(2,1)S(1)} fusion(bf16[48,4096]{1,0:T(8,128)(2,1)S(1)} %reshape.15, bf16[1,4096,1024]{2,1,0:T(8,128)(2,1)} %param.10, f32[48,1024]{1,0:T(8,128)S(1)} %fusion.4), kind=kOutput, calls=%fused_computation.9 | convolution fusion | flops 402948096 | bytes 9076736 | tf_op jit(solution)/shard_map/dot_general | solution.py:28
  50.2 0.0 copy-start
  50.3 0.0 copy-start.1
  50.3 31.6 %all_gather.11 = bf16[48,8192]{1,0:T(8,128)(2,1)S(1)} all-gather(bf16[48,1024]{1,0:T(8,128)(2,1)S(1)} %fusion.10), channel_id=1, replica_groups=mesh['expert'=4,'shard'=8] {'shard'}, dimensions={1}, use_global_device_ids=true | all-gather | bytes 884736 | tf_op jit(solution)/shard_map/all_gather | solution.py:31
  81.9 0.0 slice-done
  81.9 0.0 slice-done.1
  81.9 2.6 %fusion.13 = bf16[48,512]{1,0:T(8,128)(2,1)S(1)} fusion(bf16[48,8192]{1,0:T(8,128)(2,1)S(1)} %all_gather.11, bf16[1,512,8192]{2,1,0:T(8,128)(2,1)S(1)} %bitcast.40), kind=kOutput, calls=%fused_computation.10 | convolution fusion | flops 402677760 | bytes 9224192 | tf_op jit(solution)/shard_map/dot_general | solution.py:30
  84.6 12.8 %all_to_all.32 = bf16[8,6,512]{2,1,0:T(8,128)(2,1)} all-to-all(bf16[8,6,512]{2,1,0:T(8,128)(2,1)S(1)} %all_to_all.24), channel_id=1, replica_groups=mesh['expert'=4,'shard'=8] {'shard'}, dimensions={0} | all-to-all | bytes 98304 | tf_op jit(solution)/shard_map/all_to_all | solution.py:36
  97.4 3.3 %all-to-all-start.1 = ((bf16[6,4,1024]{2,0,1:T(8,128)(2,1)}), bf16[6,4,1024]{2,0,1:T(8,128)(2,1)S(1)}, u32[]{:S(2)}, u32[]{:S(2)}) async-start(bf16[6,4,1024]{2,0,1:T(8,128)(2,1)} %bitcast.9), calls=%async_computation.1 | async-start | bytes 131072 | tf_op jit(solution)/shard_map/all_to_all | solution.py:39
  100.7 0.0 copy-done
  100.7 0.0 copy-done.1
  100.7 4.1 %all-to-all-done.1 = bf16[6,4,1024]{2,0,1:T(8,128)(2,1)S(1)} async-done(((bf16[6,4,1024]{2,0,1:T(8,128)(2,1)}), bf16[6,4,1024]{2,0,1:T(8,128)(2,1)S(1)}, u32[]{:S(2)}, u32[]{:S(2)}) %all-to-all-start.1) | async-done | bytes 49184 | tf_op jit(solution)/shard_map/all_to_all | solution.py:39
  104.8 0.8 fusion.16
  (6 shorter events, 0.1 us)
Async XLA Ops:
  40.0 41.9 %slice-start = ((s8[8388608]{0:T(1024)(128)(4,1)}), s8[4194304]{0:T(1024)(128)(4,1)S(1)}, s32[]{:S(2)}) async-start(s8[8388608]{0:T(1024)(128)(4,1)} %bitcast.39), calls=%async_computation.2 | async-start | bytes 8388608
  45.1 36.8 %slice-start.1 = ((s8[8388608]{0:T(1024)(128)(4,1)}), s8[4194304]{0:T(1024)(128)(4,1)S(1)}, s32[]{:S(2)}) async-start(s8[8388608]{0:T(1024)(128)(4,1)} %bitcast.39), calls=%async_computation.3 | async-start | bytes 8388608
  50.2 50.4 %copy-start = (s32[6,2]{0,1:T(2,128)S(1)}, s32[6,2]{0,1:T(2,128)}, u32[]{:S(2)}) copy-start(s32[6,2]{0,1:T(2,128)} %param.7) | copy-start | bytes 148
  50.3 50.4 %copy-start.1 = (f32[6,2]{0,1:T(2,128)S(1)}, f32[6,2]{0,1:T(2,128)}, u32[]{:S(2)}) copy-start(f32[6,2]{0,1:T(2,128)} %param.8) | copy-start | bytes 148
  97.4 7.4 %all-to-all-start.1 = ((bf16[6,4,1024]{2,0,1:T(8,128)(2,1)}), bf16[6,4,1024]{2,0,1:T(8,128)(2,1)S(1)}, u32[]{:S(2)}, u32[]{:S(2)}) async-start(bf16[6,4,1024]{2,0,1:T(8,128)(2,1)} %bitcast.9), calls=%async_computation.1 | async-start | bytes 131072 | tf_op jit(solution)/shard_map/all_to_all | solution.py:39
where the time goes:
time: 106 us
  blocking collectives  83.2 us (78%)
  matrix products  13.8 us (13%)
  waiting for transfers between devices  4.05 us (4%)
  starting transfers between devices  3.28 us (3%)
    all_gather x1, blocking collectives, shards(): piece = lax.all_gather(own_rows, 'shard', axis=0, tiled=True)  32.4 us
    all_gather x1, blocking collectives, shards(): lax.all_gather(hidden, 'shard', axis=1, tiled=True)  31.6 us
    all_to_all x1, blocking collectives, shards(): lax.all_to_all(out_columns.astype(jnp.bfloat16), 'shard', split_axis=0, c...  12.8 us
    all_gather x1, blocking collectives, shards(): whole = lax.all_gather(tokens, 'expert', axis=1, tiled=True)  6.44 us
    dot_general x1, matrix products, shards(): up_out = jnp.dot(piece, up_local, preferred_element_type=jnp.float32)  5.11 us
    dot_general x1, matrix products, shards(): gate_out = jnp.dot(piece, gate_local, preferred_element_type=jnp.float32)  5.1 us
    all_to_all x1, waiting for transfers between devices, shards(): lax.all_to_all(expert_out, 'expert', split_axis=1, concat_axis=0, tiled=T...  4.05 us
    all_to_all x1, starting transfers between devices, shards(): lax.all_to_all(expert_out, 'expert', split_axis=1, concat_axis=0, tiled=T...  3.28 us
  transfers between devices with their start and end apart: 1, of which 1 were waited for; matrix products, arithmetic and copies ran while one was open for 0% of the time, Pallas kernels for 0%

commit v1 on v0

v1 whole, which is shorter than its diff:
```python
import functools

import jax
import jax.numpy as jnp
from jax import lax
from jax.experimental import pallas as pl
from jax.experimental.pallas import tpu as pltpu
from jax.sharding import PartitionSpec as P

PAD = 8
MESH = pl.DeviceIdType.MESH
F32 = jnp.float32
BF16 = jnp.bfloat16


def flip(index, mask):
    bit, out = 1, index
    while bit <= mask:
        if mask & bit:
            out = out + bit - 2 * bit * ((index // bit) % 2)
        bit *= 2
    return out


def kernel(
    n_e, n_s, chunks,
    tok_ref, ids_ref, gates_ref, gate_hbm, up_hbm, down_hbm, out_ref,
    gbuf, ubuf, dbuf, x8, xc, gacc, uacc, hbuf, oacc, obuf, rbuf,
    wsem, dsem, a_send, a_recv, e_send, e_recv, h_send, h_fwd, h_recv, c_send, c_recv,
):
    e = lax.axis_index("expert")
    s = lax.axis_index("shard")
    tok, width = tok_ref.shape
    tokens = tok * n_s
    hid = gbuf.shape[2]
    wide = hid // chunks
    rows_out = dbuf.shape[1]
    group = n_s // n_e
    n_dev = n_e * n_s

    weight_copies, down_copies = [], []
    for r in range(n_e):
        rows = pl.ds(pl.multiple_of(flip(e, r) * width, width), width)
        pair = (
            pltpu.make_async_copy(gate_hbm.at[0, rows, :], gbuf.at[r], wsem.at[0, r]),
            pltpu.make_async_copy(up_hbm.at[0, rows, :], ubuf.at[r], wsem.at[1, r]),
        )
        for copy in pair:
            copy.start()
        weight_copies.append(pair)
    for q in range(n_s):
        columns = pl.ds(pl.multiple_of(flip(s, q) * hid, hid), hid)
        copy = pltpu.make_async_copy(down_hbm.at[0, :, columns], dbuf.at[q], dsem.at[q])
        copy.start()
        down_copies.append(copy)

    x8[s] = jnp.concatenate(
        [tok_ref[...].astype(F32), jnp.zeros((PAD - tok, width), F32)], axis=0
    ).astype(BF16)
    gacc[...] = jnp.zeros_like(gacc)
    uacc[...] = jnp.zeros_like(uacc)
    oacc[...] = jnp.zeros_like(oacc)

    barrier = pltpu.get_barrier_semaphore()
    me = e * n_s + s

    def greet(i, carry):
        other = lax.rem(me + i, n_dev)
        pl.semaphore_signal(
            barrier, inc=1, device_id=(other // n_s, other % n_s), device_id_type=MESH
        )
        return carry

    lax.fori_loop(1, n_dev, greet, 0)
    pl.semaphore_wait(barrier, n_dev - 1)

    sent = []

    def remote(src, dst, send, recv, device):
        return pltpu.make_async_remote_copy(
            src_ref=src, dst_ref=dst, send_sem=send, recv_sem=recv,
            device_id=device, device_id_type=MESH,
        )

    def push(*args):
        copy = remote(*args)
        copy.start()
        sent.append(copy)

    for q in sorted(range(1, n_s), reverse=True):
        push(x8.at[s], x8.at[s], a_send.at[q], a_recv.at[q], (e, flip(s, q)))
    for q in range(1, n_s):
        other = flip(s, q)
        remote(x8.at[other], x8.at[other], a_send.at[q], a_recv.at[q], (e, other)).wait_recv()

    padded = n_s * PAD
    i = lax.broadcasted_iota(jnp.int32, (tokens, padded), 0)
    j = lax.broadcasted_iota(jnp.int32, (tokens, padded), 1)
    block = lax.shift_right_logical(j, PAD.bit_length() - 1)
    pick = ((i == j - (PAD - tok) * block) & (j - PAD * block < tok)).astype(F32).astype(BF16)
    whole = x8[...].astype(F32).reshape(padded, width).astype(BF16)
    xc[0] = jnp.dot(pick, whole, preferred_element_type=F32).astype(BF16)

    partner = (flip(e, 1), s)
    for r in range(2, n_e, 2):
        push(xc.at[0], xc.at[r], e_send.at[r], e_recv.at[r], (flip(e, r), s))
    push(xc.at[0], xc.at[1], e_send.at[1], e_recv.at[1], partner)

    def arrived(r):
        remote(xc.at[r], xc.at[r], e_send.at[r], e_recv.at[r], partner).wait_recv()

    def project(r, last):
        for copy in weight_copies[r]:
            copy.wait()
        for c in range(chunks):
            columns = slice(c * wide, (c + 1) * wide)
            g = gacc[:, columns] + jnp.dot(xc[r], gbuf[r, :, columns], preferred_element_type=F32)
            u = uacc[:, columns] + jnp.dot(xc[r], ubuf[r, :, columns], preferred_element_type=F32)
            if not last:
                gacc[:, columns] = g
                uacc[:, columns] = u
                continue
            hbuf[0, c] = (g / (1.0 + jnp.exp(-g)) * u).astype(BF16)
            push(hbuf.at[0, c], hbuf.at[1, c], h_fwd.at[0, c], h_recv.at[1, c], (e, flip(s, 1)))
            for q in range(2, n_s, 2):
                push(hbuf.at[0, c], hbuf.at[q, c], h_send.at[q, c], h_recv.at[q, c], (e, flip(s, q)))

    project(0, n_e == 1)
    arrived(1)
    project(1, n_e == 2)
    for r in range(2, n_e, 2):
        arrived(r)
        push(xc.at[r], xc.at[r + 1], e_send.at[r + 1], e_recv.at[r + 1], partner)
        project(r, False)
    for r in range(3, n_e, 2):
        arrived(r)
        project(r, r == n_e - 1)

    waited = set()

    def down(q, c):
        if q not in waited:
            down_copies[q].wait()
            waited.add(q)
        oacc[...] += lax.dot_general(
            hbuf[q, c], dbuf[q, :, c * wide:(c + 1) * wide], (((1,), (1,)), ((), ())),
            preferred_element_type=F32,
        )

    def landed(q, c):
        remote(hbuf.at[q, c], hbuf.at[q, c], h_send.at[q, c], h_recv.at[q, c], partner).wait_recv()

    for c in range(chunks):
        down(0, c)
    for c in range(chunks):
        for q in range(2, n_s, 2):
            landed(q, c)
            push(hbuf.at[q, c], hbuf.at[q + 1, c], h_fwd.at[q, c], h_recv.at[q + 1, c], (e, flip(s, 1)))
            down(q, c)
        landed(1, c)
        down(1, c)
    for c in range(chunks):
        for q in range(3, n_s, 2):
            landed(q, c)
            down(q, c)

    spread = jnp.where((i == j - (PAD - tok) * block) & (j - PAD * block < tok), 1.0, 0.0).T.astype(BF16)
    blocks = jnp.dot(spread, oacc[...].astype(BF16), preferred_element_type=F32)
    obuf[...] = blocks.reshape(n_s, PAD, rows_out).astype(BF16)
    owner = s // group
    slot = e * group + lax.rem(s, group)
    own = e == owner

    @pl.when(own)
    def _():
        keep = pltpu.make_async_copy(obuf.at[s], rbuf.at[slot], c_recv.at[slot])
        keep.start()

    @pl.when(jnp.logical_not(own))
    def _():
        remote(obuf.at[s], rbuf.at[slot], c_send.at[0], c_recv.at[slot], (owner, s)).start()

    for q in range(1, n_s):
        other = flip(s, q)
        push(obuf.at[other], rbuf.at[slot], c_send.at[q], c_recv.at[slot], (owner, other))

    ids = ids_ref[...]
    gates = gates_ref[...]
    for copy in sent[:len(sent) - (n_s - 1)]:
        copy.wait_send()
    totals = [jnp.zeros((tok, rows_out), F32) for _ in range(group)]
    for x in range(n_e):
        weight = jnp.sum(jnp.where(ids == x, gates, 0.0), axis=1, keepdims=True)
        for k in range(group):
            n = x * group + k
            remote(rbuf.at[n], rbuf.at[n], c_send.at[0], c_recv.at[n], partner).wait_recv()
            totals[k] = totals[k] + weight * rbuf[n].astype(F32)[:tok]
    for k in range(group):
        out_ref[:, k * rows_out:(k + 1) * rows_out] = totals[k].astype(BF16)

    @pl.when(jnp.logical_not(own))
    def _():
        remote(obuf.at[s], rbuf.at[slot], c_send.at[0], c_recv.at[slot], (owner, s)).wait_send()

    for copy in sent[len(sent) - (n_s - 1):]:
        copy.wait_send()


def shards(n_e, n_s, tokens, expert_ids, gates, gate_proj, up_proj, down_proj_t):
    tok, width = tokens.shape
    _, _, hid = gate_proj.shape
    _, rows_out, _ = down_proj_t.shape
    chunks = max(1, hid // 256)
    wide = hid // chunks
    total = tok * n_s
    group = n_s // n_e
    dma = pltpu.SemaphoreType.DMA
    vmem = pl.BlockSpec(memory_space=pltpu.VMEM)
    hbm = pl.BlockSpec(memory_space=pl.ANY)
    return pl.pallas_call(
        functools.partial(kernel, n_e, n_s, chunks),
        out_shape=jax.ShapeDtypeStruct((tok, width), BF16),
        in_specs=[vmem, vmem, vmem, hbm, hbm, hbm],
        out_specs=vmem,
        scratch_shapes=[
            pltpu.VMEM((n_e, width, hid), BF16),
            pltpu.VMEM((n_e, width, hid), BF16),
            pltpu.VMEM((n_s, rows_out, hid), BF16),
            pltpu.VMEM((n_s, PAD, width), BF16),
            pltpu.VMEM((n_e, total, width), BF16),
            pltpu.VMEM((total, hid), F32),
            pltpu.VMEM((total, hid), F32),
            pltpu.VMEM((n_s, chunks, total, wide), BF16),
            pltpu.VMEM((total, rows_out), F32),
            pltpu.VMEM((n_s, PAD, rows_out), BF16),
            pltpu.VMEM((n_e * group, PAD, rows_out), BF16),
            dma((2, n_e)),
            dma((n_s,)),
            dma((n_s,)),
            dma((n_s,)),
            dma((n_e,)),
            dma((n_e,)),
            dma((n_s, chunks)),
            dma((n_s, chunks)),
            dma((n_s, chunks)),
            dma((n_s,)),
            dma((n_e * group,)),
        ],
        compiler_params=pltpu.CompilerParams(
            collective_id=0, has_side_effects=True, vmem_limit_bytes=60 * 1024 * 1024
        ),
    )(tokens, expert_ids, gates, gate_proj, up_proj, down_proj_t)


def solution(mesh):
    in_specs = (
        P("shard", "expert"),
        P("shard", None),
        P("shard", None),
        P("expert", None, "shard"),
        P("expert", None, "shard"),
        P("expert", "shard", None),
    )
    out_specs = P("shard", "expert")
    body = functools.partial(shards, mesh.shape["expert"], mesh.shape["shard"])
    return jax.shard_map(body, mesh=mesh, in_specs=in_specs, out_specs=out_specs, check_vma=False)
```

time: 106 us -> 41.2 us (0.39)
  blocking collectives: 83.2 us -> 0 us
  Pallas kernels: 0 us -> 36.9 us
  matrix products: 13.8 us -> 0 us
  waiting for transfers between devices: 4.05 us -> 0 us
  local copies, waits for them, and re-layouts: 0.18 us -> 4.02 us
  starting transfers between devices: 3.28 us -> 0 us
    all_gather x3 -> x0, blocking collectives: 70.4 us -> none  [the longest x1 32.4 us: shards(): piece = lax.all_gather(own_rows, 'shard', axis=0, tiled=True)]
    pallas_call x0 -> x1, Pallas kernels: none -> 36.9 us  [shards(): pl.pallas_call(functools.partial(kernel, n_e, n_s, chunks), out_shape=jax...]
    dot_general x5 -> x0, matrix products: 13.8 us -> none  [the longest x1 5.11 us: shards(): up_out = jnp.dot(piece, up_local, preferred_element_type=jnp.float32)]
    all_to_all x1 -> x0, blocking collectives: 12.8 us -> none  [shards(): lax.all_to_all(out_columns.astype(jnp.bfloat16), 'shard', split_axis=0, c...]
    all_to_all x1 -> x0, waiting for transfers between devices: 4.05 us -> none  [shards(): lax.all_to_all(expert_out, 'expert', split_axis=1, concat_axis=0, tiled=T...]
    unnamed x9 -> x3, local copies, waits for them, and re-layouts: 0.16 us -> 4.02 us
    all_to_all x1 -> x0, starting transfers between devices: 3.28 us -> none  [shards(): lax.all_to_all(expert_out, 'expert', split_axis=1, concat_axis=0, tiled=T...]
  transfers between devices with their start and end apart: 1 -> 0, of which waited for: 1 -> 0; matrix products, arithmetic and copies ran while one was open for 0% -> 0% of each run, Pallas kernels for 0% -> 0%
where the time goes in v1:
time: 41.2 us; the launch traced here: 40.9 us
  Pallas kernels  36.9 us (90%)
  local copies, waits for them, and re-layouts  4.02 us (10%)
    pallas_call x1, Pallas kernels, shards(): pl.pallas_call(functools.partial(kernel, n_e, n_s, chunks), out_shape=jax...  36.9 us
    unnamed x3, local copies, waits for them, and re-layouts  4.02 us

profile of v1, /device:TPU:0, one launch (start us, length us, event | category | flops | bytes accessed | tf_op | source)
XLA Modules:
  0.0 40.9 jit_solution(5409488112642696884)
XLA Ops:
  0.0 1.4 %copy.7.ids_ref = s32[6,2]{1,0:T(8,128)} copy(s32[6,2]{0,1:T(2,128)} %param.7) | data formatting | bytes 96 | tf_op args[1]
  1.4 1.3 %copy.8.gates_ref = f32[6,2]{1,0:T(8,128)} copy(f32[6,2]{0,1:T(2,128)} %param.8) | data formatting | bytes 96 | tf_op args[2]
  2.7 36.9 %shard_map.64 = bf16[6,1024]{1,0:T(8,128)(2,1)} custom-call(bf16[6,1024]{1,0:T(8,128)(2,1)} %tok_ref.1, s32[6,2]{1,0:T(8,128)} %copy.7.ids_ref, f32[6,2]{1,0:T(8,128)} %copy.8.gates_ref, bf16[1,4096,1024]{2,1,0:T(8,128)(2,1)} %gate_hbm.1, bf16[1,4096,1024]{2,1,0:T(8,128)(2,1)} %up_hbm.1, bf16[1,512,8192]{2,1,0:T(8,128)(2,1)} %down_hbm.1), custom_call_target="tpu_custom_call" | custom-call | tf_op jit(solution)/shard_map/pallas_call | solution.py:220
  39.6 1.3 %copy.10 = bf16[6,1024]{1,0:T(8,128)(2,1)} copy(bf16[6,1024]{1,0:T(8,128)(2,1)} %shard_map.64) | data formatting | bytes 24576

commit v2 on v1

--- a/solution.py
+++ b/solution.py
@@ -25,8 +25,8 @@
 def kernel(
     n_e, n_s, chunks,
     tok_ref, ids_ref, gates_ref, gate_hbm, up_hbm, down_hbm, out_ref,
-    gbuf, ubuf, dbuf, x8, xc, gacc, uacc, hbuf, oacc, obuf, rbuf,
-    wsem, dsem, a_send, a_recv, e_send, e_recv, h_send, h_fwd, h_recv, c_send, c_recv,
+    gbuf, ubuf, dbuf, x8, gacc, uacc, hbuf, oacc, obuf, rbuf,
+    wsem, dsem, a_send, a_recv, h_send, h_fwd, h_recv, c_send, c_recv,
 ):
     e = lax.axis_index("expert")
     s = lax.axis_index("shard")
@@ -49,12 +49,12 @@
             copy.start()
         weight_copies.append(pair)
     for q in range(n_s):
-        columns = pl.ds(pl.multiple_of(flip(s, q) * hid, hid), hid)
+        columns = slice(q * hid, (q + 1) * hid)
         copy = pltpu.make_async_copy(down_hbm.at[0, :, columns], dbuf.at[q], dsem.at[q])
         copy.start()
         down_copies.append(copy)
 
-    x8[s] = jnp.concatenate(
+    x8[0, s] = jnp.concatenate(
         [tok_ref[...].astype(F32), jnp.zeros((PAD - tok, width), F32)], axis=0
     ).astype(BF16)
     gacc[...] = jnp.zeros_like(gacc)
@@ -87,84 +87,143 @@
         copy.start()
         sent.append(copy)
 
+    partner = (flip(e, 1), s)
+
+    def onward(block):
+        for r in range(2, n_e, 2):
+            push(x8.at[0, block], x8.at[r, block], a_send.at[r, block], a_recv.at[r, block], (flip(e, r), s))
+        push(x8.at[0, block], x8.at[1, block], a_send.at[1, block], a_recv.at[1, block], partner)
+
+    def arrived(r, block):
+        view = x8.at[r, block]
+        remote(view, view, a_send.at[r, block], a_recv.at[r, block], partner).wait_recv()
+
     for q in sorted(range(1, n_s), reverse=True):
-        push(x8.at[s], x8.at[s], a_send.at[q], a_recv.at[q], (e, flip(s, q)))
+        push(x8.at[0, s], x8.at[0, s], a_send.at[0, flip(s, q)], a_recv.at[0, s], (e, flip(s, q)))
+    onward(s)
     for q in range(1, n_s):
-        other = flip(s, q)
-        remote(x8.at[other], x8.at[other], a_send.at[q], a_recv.at[q], (e, other)).wait_recv()
+        block = flip(s, q)
+        arrived(0, block)
+        onward(block)
 
     padded = n_s * PAD
     i = lax.broadcasted_iota(jnp.int32, (tokens, padded), 0)
     j = lax.broadcasted_iota(jnp.int32, (tokens, padded), 1)
-    block = lax.shift_right_logical(j, PAD.bit_length() - 1)
-    pick = ((i == j - (PAD - tok) * block) & (j - PAD * block < tok)).astype(F32).astype(BF16)
-    whole = x8[...].astype(F32).reshape(padded, width).astype(BF16)
-    xc[0] = jnp.dot(pick, whole, preferred_element_type=F32).astype(BF16)
-
-    partner = (flip(e, 1), s)
-    for r in range(2, n_e, 2):
-        push(xc.at[0], xc.at[r], e_send.at[r], e_recv.at[r], (flip(e, r), s))
-    push(xc.at[0], xc.at[1], e_send.at[1], e_recv.at[1], partner)
-
-    def arrived(r):
-        remote(xc.at[r], xc.at[r], e_send.at[r], e_recv.at[r], partner).wait_recv()
+    block_of = lax.shift_right_logical(j, PAD.bit_length() - 1)
+    pick = ((i == j - (PAD - tok) * block_of) & (j - PAD * block_of < tok)).astype(F32).astype(BF16)
+    line, side = s // 2, lax.rem(s, 2)
+    across = (e, flip(s, 1))
+    n_line = n_s // 2
+
+    def send_along(place, c, step, k):
+        beside = line + step
+
+        @pl.when((beside >= 0) & (beside < n_line))
+        def _():
+            remote(hbuf.at[place, c], hbuf.at[place, c], h_send.at[k, place, c], h_recv.at[place, c],
+                   (e, s + 2 * step)).start()
+
+    def send_across(place, c):
+        remote(hbuf.at[place, c], hbuf.at[place, c], h_fwd.at[place, c], h_recv.at[place, c], across).start()
 
     def project(r, last):
+        whole = x8[r].astype(F32).reshape(padded, width).astype(BF16)
+        rows = jnp.dot(pick, whole, preferred_element_type=F32).astype(BF16)
         for copy in weight_copies[r]:
             copy.wait()
         for c in range(chunks):
             columns = slice(c * wide, (c + 1) * wide)
-            g = gacc[:, columns] + jnp.dot(xc[r], gbuf[r, :, columns], preferred_element_type=F32)
-            u = uacc[:, columns] + jnp.dot(xc[r], ubuf[r, :, columns], preferred_element_type=F32)
+            g = gacc[:, columns] + jnp.dot(rows, gbuf[r, :, columns], preferred_element_type=F32)
+            u = uacc[:, columns] + jnp.dot(rows, ubuf[r, :, columns], preferred_element_type=F32)
             if not last:
                 gacc[:, columns] = g
                 uacc[:, columns] = u
                 continue
-            hbuf[0, c] = (g / (1.0 + jnp.exp(-g)) * u).astype(BF16)
-            push(hbuf.at[0, c], hbuf.at[1, c], h_fwd.at[0, c], h_recv.at[1, c], (e, flip(s, 1)))
-            for q in range(2, n_s, 2):
-                push(hbuf.at[0, c], hbuf.at[q, c], h_send.at[q, c], h_recv.at[q, c], (e, flip(s, q)))
+            hbuf[s, c] = (g / (1.0 + jnp.exp(-g)) * u).astype(BF16)
+            send_across(s, c)
+            send_along(s, c, 1, 0)
+            send_along(s, c, -1, 1)
 
     project(0, n_e == 1)
-    arrived(1)
+    for q in range(n_s):
+        arrived(1, flip(s, q))
     project(1, n_e == 2)
     for r in range(2, n_e, 2):
-        arrived(r)
-        push(xc.at[r], xc.at[r + 1], e_send.at[r + 1], e_recv.at[r + 1], partner)
+        for q in range(n_s):
+            block = flip(s, q)
+            arrived(r, block)
+            push(x8.at[r, block], x8.at[r + 1, block], a_send.at[r + 1, block], a_recv.at[r + 1, block], partner)
         project(r, False)
     for r in range(3, n_e, 2):
-        arrived(r)
+        for q in range(n_s):
+            arrived(r, flip(s, q))
         project(r, r == n_e - 1)
 
-    waited = set()
-
-    def down(q, c):
-        if q not in waited:
-            down_copies[q].wait()
-            waited.add(q)
+    for copy in down_copies:
+        copy.wait()
+
+    def down(place, c):
+        columns = pl.ds(pl.multiple_of(c * wide, wide), wide)
         oacc[...] += lax.dot_general(
-            hbuf[q, c], dbuf[q, :, c * wide:(c + 1) * wide], (((1,), (1,)), ((), ())),
+            hbuf[place, c], dbuf[place, :, columns], (((1,), (1,)), ((), ())),
             preferred_element_type=F32,
         )
 
-    def landed(q, c):
-        remote(hbuf.at[q, c], hbuf.at[q, c], h_send.at[q, c], h_recv.at[q, c], partner).wait_recv()
+    def landed(place, c):
+        view = hbuf.at[place, c]
+        remote(view, view, h_fwd.at[place, c], h_recv.at[place, c], across).wait_recv()
+
+    inner = jnp.minimum(line, n_line - 1 - line)
+    roomy = 1 - 2 * (line // ((n_line + 1) // 2))
+
+    def event(t):
+        paired = t < 2 * inner * chunks
+        late = t - 2 * inner * chunks
+        pair = t // 2
+        away = jnp.where(paired, pair // chunks + 1, inner + 1 + late // chunks)
+        c = jnp.where(paired, lax.rem(pair, chunks), lax.rem(late, chunks))
+        sign = jnp.where(paired, 1 - 2 * lax.rem(t, 2), roomy)
+        return line + sign * away, c, sign
 
     for c in range(chunks):
-        down(0, c)
-    for c in range(chunks):
-        for q in range(2, n_s, 2):
-            landed(q, c)
-            push(hbuf.at[q, c], hbuf.at[q + 1, c], h_fwd.at[q, c], h_recv.at[q + 1, c], (e, flip(s, 1)))
-            down(q, c)
-        landed(1, c)
-        down(1, c)
-    for c in range(chunks):
-        for q in range(3, n_s, 2):
-            landed(q, c)
-            down(q, c)
-
-    spread = jnp.where((i == j - (PAD - tok) * block) & (j - PAD * block < tok), 1.0, 0.0).T.astype(BF16)
+        down(s, c)
+
+    steps = (n_line - 1) * chunks
+    first = min(chunks, steps)
+
+    def along(t):
+        spot, c, sign = event(t)
+        place = 2 * spot + side
+        landed(place, c)
+        send_along(place, c, -sign, 0)
+        send_across(place, c)
+        down(place, c)
+
+    def beside_own(c):
+        landed(flip(s, 1), c)
+        down(flip(s, 1), c)
+
+    def beside(t):
+        spot, c, _ = event(t)
+        place = 2 * spot + 1 - side
+        landed(place, c)
+        down(place, c)
+
+    @pl.loop(0, first)
+    def _(t):
+        along(t)
+        beside_own(t)
+
+    @pl.loop(first, steps)
+    def _(t):
+        along(t)
+        beside(t - first)
+
+    @pl.loop(steps - first, steps)
+    def _(t):
+        beside(t)
+
+    spread = pick.astype(F32).T.astype(BF16)
     blocks = jnp.dot(spread, oacc[...].astype(BF16), preferred_element_type=F32)
     obuf[...] = blocks.reshape(n_s, PAD, rows_out).astype(BF16)
     owner = s // group
@@ -186,11 +245,38 @@
 
     ids = ids_ref[...]
     gates = gates_ref[...]
+    diagonal = lax.broadcasted_iota(jnp.int32, (tok, tok), 0) == lax.broadcasted_iota(jnp.int32, (tok, tok), 1)
     for copy in sent[:len(sent) - (n_s - 1)]:
         copy.wait_send()
+
+    @pl.loop(0, chunks)
+    def _(c):
+        for k, step in ((0, 1), (1, -1)):
+            beside_me = line + step
+
+            @pl.when((beside_me >= 0) & (beside_me < n_line))
+            def _():
+                remote(hbuf.at[s, c], hbuf.at[s, c], h_send.at[k, s, c], h_recv.at[s, c], across).wait_send()
+
+        remote(hbuf.at[s, c], hbuf.at[s, c], h_fwd.at[s, c], h_recv.at[s, c], across).wait_send()
+
+    @pl.loop(0, steps)
+    def _(t):
+        spot, c, sign = event(t)
+        place = 2 * spot + side
+        view = hbuf.at[place, c]
+        beside_me = line - sign
+
+        @pl.when((beside_me >= 0) & (beside_me < n_line))
+        def _():
+            remote(view, view, h_send.at[0, place, c], h_recv.at[place, c], across).wait_send()
+
+        remote(view, view, h_fwd.at[place, c], h_recv.at[place, c], across).wait_send()
+
     totals = [jnp.zeros((tok, rows_out), F32) for _ in range(group)]
     for x in range(n_e):
-        weight = jnp.sum(jnp.where(ids == x, gates, 0.0), axis=1, keepdims=True)
+        row = jnp.sum(jnp.where(ids == x, gates, 0.0), axis=0, keepdims=True)
+        weight = jnp.sum(jnp.where(diagonal, row, 0.0), axis=1, keepdims=True)
         for k in range(group):
             n = x * group + k
             remote(rbuf.at[n], rbuf.at[n], c_send.at[0], c_recv.at[n], partner).wait_recv()
@@ -226,8 +312,7 @@
             pltpu.VMEM((n_e, width, hid), BF16),
             pltpu.VMEM((n_e, width, hid), BF16),
             pltpu.VMEM((n_s, rows_out, hid), BF16),
-            pltpu.VMEM((n_s, PAD, width), BF16),
-            pltpu.VMEM((n_e, total, width), BF16),
+            pltpu.VMEM((n_e, n_s, PAD, width), BF16),
             pltpu.VMEM((total, hid), F32),
             pltpu.VMEM((total, hid), F32),
             pltpu.VMEM((n_s, chunks, total, wide), BF16),
@@ -236,11 +321,9 @@
             pltpu.VMEM((n_e * group, PAD, rows_out), BF16),
             dma((2, n_e)),
             dma((n_s,)),
-            dma((n_s,)),
-            dma((n_s,)),
-            dma((n_e,)),
-            dma((n_e,)),
-            dma((n_s, chunks)),
+            dma((n_e, n_s)),
+            dma((n_e, n_s)),
+            dma((2, n_s, chunks)),
             dma((n_s, chunks)),
             dma((n_s, chunks)),
             dma((n_s,)),
@@ -249,7 +332,7 @@
         compiler_params=pltpu.CompilerParams(
             collective_id=0, has_side_effects=True, vmem_limit_bytes=60 * 1024 * 1024
         ),
-    )(tokens, expert_ids, gates, gate_proj, up_proj, down_proj_t)
+    )(tokens, expert_ids.T, gates.T, gate_proj, up_proj, down_proj_t)
 
 
 def solution(mesh):

time: 41.2 us -> 40.8 us (level)
  local copies, waits for them, and re-layouts: 4.02 us -> 1.32 us
  Pallas kernels: 36.9 us -> 39.2 us
    unnamed x3 -> x1, local copies, waits for them, and re-layouts: 4.02 us -> 1.32 us
    pallas_call x1, Pallas kernels: 36.9 us -> 39.2 us  [shards(): pl.pallas_call(functools.partial(kernel, n_e, n_s, chunks), out_shape=jax...]
where the time goes in v2:
time: 40.8 us; the launch traced here: 40.6 us
  Pallas kernels  39.2 us (96%)
  local copies, waits for them, and re-layouts  1.32 us (3%)
    pallas_call x1, Pallas kernels, shards(): pl.pallas_call(functools.partial(kernel, n_e, n_s, chunks), out_shape=jax...  39.2 us
    unnamed x1, local copies, waits for them, and re-layouts  1.32 us

profile of v2, /device:TPU:0, one launch (start us, length us, event | category | flops | bytes accessed | tf_op | source)
XLA Modules:
  0.0 40.6 jit_solution(14628697330794712893)
XLA Ops:
  0.0 39.2 %shard_map.64 = bf16[6,1024]{1,0:T(8,128)(2,1)} custom-call(bf16[6,1024]{1,0:T(8,128)(2,1)} %tok_ref.1, s32[2,6]{1,0:T(2,128)} %bitcast.2, f32[2,6]{1,0:T(2,128)} %bitcast.3, bf16[1,4096,1024]{2,1,0:T(8,128)(2,1)} %gate_hbm.1, bf16[1,4096,1024]{2,1,0:T(8,128)(2,1)} %up_hbm.1, bf16[1,512,8192]{2,1,0:T(8,128)(2,1)} %down_hbm.1), custom_call_target="tpu_custom_call" | custom-call | tf_op jit(solution)/shard_map/pallas_call | solution.py:306
  39.2 1.3 %copy.8 = bf16[6,1024]{1,0:T(8,128)(2,1)} copy(bf16[6,1024]{1,0:T(8,128)(2,1)} %shard_map.64) | data formatting | bytes 24576

commit v3 on v2

--- a/solution.py
+++ b/solution.py
@@ -185,43 +185,71 @@
         sign = jnp.where(paired, 1 - 2 * lax.rem(t, 2), roomy)
         return line + sign * away, c, sign
 
-    for c in range(chunks):
-        down(s, c)
-
     steps = (n_line - 1) * chunks
-    first = min(chunks, steps)
-
-    def along(t):
+
+    def across_piece(t):
+        spot, c, _ = event(t)
+        return 2 * spot + 1 - side, c
+
+    def along_piece(t):
+        spot, c, _ = event(t)
+        return 2 * spot + side, c
+
+    def together(pieces, wait):
+        total = oacc[...]
+        for place, c in pieces:
+            if wait:
+                landed(place, c)
+            columns = pl.ds(pl.multiple_of(c * wide, wide), wide)
+            total += lax.dot_general(
+                hbuf[place, c], dbuf[place, :, columns], (((1,), (1,)), ((), ())),
+                preferred_element_type=F32,
+            )
+        oacc[...] = total
+
+    def relay(t):
         spot, c, sign = event(t)
         place = 2 * spot + side
         landed(place, c)
         send_along(place, c, -sign, 0)
         send_across(place, c)
-        down(place, c)
-
-    def beside_own(c):
+
+    first = min(chunks, steps)
+
+    @pl.loop(0, first)
+    def _(t):
+        relay(t)
+        down(s, t)
+
+    for c in range(first, chunks):
+        down(s, c)
+
+    second = min(2 * chunks, steps)
+
+    @pl.loop(first, second)
+    def _(t):
+        relay(t)
+        landed(flip(s, 1), t - first)
+        down(flip(s, 1), t - first)
+
+    for c in range(second - first, chunks):
         landed(flip(s, 1), c)
         down(flip(s, 1), c)
 
-    def beside(t):
-        spot, c, _ = event(t)
-        place = 2 * spot + 1 - side
-        landed(place, c)
-        down(place, c)
-
-    @pl.loop(0, first)
+    @pl.loop(second, steps)
     def _(t):
-        along(t)
-        beside_own(t)
-
-    @pl.loop(first, steps)
-    def _(t):
-        along(t)
-        beside(t - first)
-
-    @pl.loop(steps - first, steps)
-    def _(t):
-        beside(t)
+        relay(t)
+        down(*along_piece(t - second))
+
+    done = (steps - second) // chunks
+
+    @pl.loop(done, n_line - 1)
+    def _(k):
+        together([along_piece(k * chunks + c) for c in range(chunks)], False)
+
+    @pl.loop(0, n_line - 1)
+    def _(k):
+        together([across_piece(k * chunks + c) for c in range(chunks)], True)
 
     spread = pick.astype(F32).T.astype(BF16)
     blocks = jnp.dot(spread, oacc[...].astype(BF16), preferred_element_type=F32)

time: 40.8 us -> 38.6 us (0.946)
  Pallas kernels: 39.2 us -> 37 us
    pallas_call x1, Pallas kernels: 39.2 us -> 37 us  [shards(): pl.pallas_call(functools.partial(kernel, n_e, n_s, chunks), out_shape=jax...]
where the time goes in v3:
time: 38.6 us; the launch traced here: 38.4 us
  Pallas kernels  37 us (96%)
  local copies, waits for them, and re-layouts  1.32 us (3%)
    pallas_call x1, Pallas kernels, shards(): pl.pallas_call(functools.partial(kernel, n_e, n_s, chunks), out_shape=jax...  37 us
    unnamed x1, local copies, waits for them, and re-layouts  1.32 us

profile of v3, /device:TPU:0, one launch (start us, length us, event | category | flops | bytes accessed | tf_op | source)
XLA Modules:
  0.0 38.4 jit_solution(17222897517057347618)
XLA Ops:
  0.0 37.0 %shard_map.64 = bf16[6,1024]{1,0:T(8,128)(2,1)} custom-call(bf16[6,1024]{1,0:T(8,128)(2,1)} %tok_ref.1, s32[2,6]{1,0:T(2,128)} %bitcast.2, f32[2,6]{1,0:T(2,128)} %bitcast.3, bf16[1,4096,1024]{2,1,0:T(8,128)(2,1)} %gate_hbm.1, bf16[1,4096,1024]{2,1,0:T(8,128)(2,1)} %up_hbm.1, bf16[1,512,8192]{2,1,0:T(8,128)(2,1)} %down_hbm.1), custom_call_target="tpu_custom_call" | custom-call | tf_op jit(solution)/shard_map/pallas_call | solution.py:334
  37.1 1.3 %copy.8 = bf16[6,1024]{1,0:T(8,128)(2,1)} copy(bf16[6,1024]{1,0:T(8,128)(2,1)} %shard_map.64) | data formatting | bytes 24576

commit v4 on v3

--- a/solution.py
+++ b/solution.py
@@ -54,9 +54,7 @@
         copy.start()
         down_copies.append(copy)
 
-    x8[0, s] = jnp.concatenate(
-        [tok_ref[...].astype(F32), jnp.zeros((PAD - tok, width), F32)], axis=0
-    ).astype(BF16)
+    x8[0, s, :tok, :] = tok_ref[...]
     gacc[...] = jnp.zeros_like(gacc)
     uacc[...] = jnp.zeros_like(uacc)
     oacc[...] = jnp.zeros_like(oacc)
@@ -89,17 +87,20 @@
 
     partner = (flip(e, 1), s)
 
+    def filled(r, block):
+        return x8.at[r, block, pl.ds(0, tok)]
+
     def onward(block):
         for r in range(2, n_e, 2):
-            push(x8.at[0, block], x8.at[r, block], a_send.at[r, block], a_recv.at[r, block], (flip(e, r), s))
-        push(x8.at[0, block], x8.at[1, block], a_send.at[1, block], a_recv.at[1, block], partner)
+            push(filled(0, block), filled(r, block), a_send.at[r, block], a_recv.at[r, block], (flip(e, r), s))
+        push(filled(0, block), filled(1, block), a_send.at[1, block], a_recv.at[1, block], partner)
 
     def arrived(r, block):
-        view = x8.at[r, block]
+        view = filled(r, block)
         remote(view, view, a_send.at[r, block], a_recv.at[r, block], partner).wait_recv()
 
     for q in sorted(range(1, n_s), reverse=True):
-        push(x8.at[0, s], x8.at[0, s], a_send.at[0, flip(s, q)], a_recv.at[0, s], (e, flip(s, q)))
+        push(filled(0, s), filled(0, s), a_send.at[0, flip(s, q)], a_recv.at[0, s], (e, flip(s, q)))
     onward(s)
     for q in range(1, n_s):
         block = flip(s, q)
@@ -111,6 +112,7 @@
     j = lax.broadcasted_iota(jnp.int32, (tokens, padded), 1)
     block_of = lax.shift_right_logical(j, PAD.bit_length() - 1)
     pick = ((i == j - (PAD - tok) * block_of) & (j - PAD * block_of < tok)).astype(F32).astype(BF16)
+    real = lax.rem(lax.broadcasted_iota(jnp.int32, (padded, width), 0), PAD) < tok
     line, side = s // 2, lax.rem(s, 2)
     across = (e, flip(s, 1))
     n_line = n_s // 2
@@ -127,7 +129,7 @@
         remote(hbuf.at[place, c], hbuf.at[place, c], h_fwd.at[place, c], h_recv.at[place, c], across).start()
 
     def project(r, last):
-        whole = x8[r].astype(F32).reshape(padded, width).astype(BF16)
+        whole = jnp.where(real, x8[r].astype(F32).reshape(padded, width), 0.0).astype(BF16)
         rows = jnp.dot(pick, whole, preferred_element_type=F32).astype(BF16)
         for copy in weight_copies[r]:
             copy.wait()
@@ -152,7 +154,7 @@
         for q in range(n_s):
             block = flip(s, q)
             arrived(r, block)
-            push(x8.at[r, block], x8.at[r + 1, block], a_send.at[r + 1, block], a_recv.at[r + 1, block], partner)
+            push(filled(r, block), filled(r + 1, block), a_send.at[r + 1, block], a_recv.at[r + 1, block], partner)
         project(r, False)
     for r in range(3, n_e, 2):
         for q in range(n_s):

time: 38.6 us -> 37.5 us (0.972)
  Pallas kernels: 37 us -> 35.9 us
    pallas_call x1, Pallas kernels: 37 us -> 35.9 us  [shards(): pl.pallas_call(functools.partial(kernel, n_e, n_s, chunks), out_shape=jax...]
where the time goes in v4:
time: 37.5 us; the launch traced here: 37.3 us
  Pallas kernels  35.9 us (96%)
  local copies, waits for them, and re-layouts  1.32 us (4%)
    pallas_call x1, Pallas kernels, shards(): pl.pallas_call(functools.partial(kernel, n_e, n_s, chunks), out_shape=jax...  35.9 us
    unnamed x1, local copies, waits for them, and re-layouts  1.32 us

profile of v4, /device:TPU:0, one launch (start us, length us, event | category | flops | bytes accessed | tf_op | source)
XLA Modules:
  0.0 37.3 jit_solution(13595168304782594981)
XLA Ops:
  0.0 35.9 %shard_map.64 = bf16[6,1024]{1,0:T(8,128)(2,1)} custom-call(bf16[6,1024]{1,0:T(8,128)(2,1)} %tok_ref.1, s32[2,6]{1,0:T(2,128)} %bitcast.2, f32[2,6]{1,0:T(2,128)} %bitcast.3, bf16[1,4096,1024]{2,1,0:T(8,128)(2,1)} %gate_hbm.1, bf16[1,4096,1024]{2,1,0:T(8,128)(2,1)} %up_hbm.1, bf16[1,512,8192]{2,1,0:T(8,128)(2,1)} %down_hbm.1), custom_call_target="tpu_custom_call" | custom-call | tf_op jit(solution)/shard_map/pallas_call | solution.py:336
  35.9 1.3 %copy.8 = bf16[6,1024]{1,0:T(8,128)(2,1)} copy(bf16[6,1024]{1,0:T(8,128)(2,1)} %shard_map.64) | data formatting | bytes 24576
